TPU v7x, 128 devices: a whole 4x4x4 slice. The times are simulated.
128 devices in a mesh: pts: 128 (over z, y, x, core).
Axes of the slice: x: 4, y: 4, z: 4, core: 2. Of those that a mesh axis runs over, the one named last changes fastest.
Arguments:
- points: bfloat16 [65536, 64], P('pts'), may hold values from -10 to 10, as said below
- targets: float32 [65536], P('pts'), may hold values from -6 to 6
- ridge_weight: float32 [], replicated, may hold values from 0.5 to 4
Outputs:
- coefficients: float32 [65536], P('pts')
- residual: float32 [65536], P('pts')
Inputs may be any that keep to these rules, and one draw needn't show every extreme that they name: `points`: each point lies near one of 1365 cluster centres; every coordinate is within -10 and 10.
All inputs are finite; a program needn't handle non-finite values.
Results may differ from a plain program's by a relative error of at most 0.005.
Values may be sent and summed in bfloat16 or wider, within the bound.
A program may use at most 192 MiB of HBM per device.

v0:
```python
import jax
import jax.numpy as jnp
from jax import lax
from jax.sharding import PartitionSpec as P

ITERS = 2


def over_all(shard, axis, dim, absorb, state):
    everything = jax.tree.map(lambda a: lax.all_gather(a, axis, axis=dim, tiled=True), shard)
    return absorb(state, everything, jnp.int32(0))


def kernel_times(own_points, own_norms, shard_rows, coef_part, inverse_width):
    widened = shard_rows.astype(jnp.float32)
    shard_norms = jnp.sum(widened * widened, axis=1)
    cross_term = jnp.dot(own_points, shard_rows.T, preferred_element_type=jnp.float32)
    distance = own_norms[:, None] + shard_norms[None, :] - 2.0 * cross_term
    kernel = jnp.exp(-inverse_width * distance).astype(jnp.bfloat16)
    return jnp.dot(kernel, coef_part, preferred_element_type=jnp.float32)


def apply_operator(direction, points, own_norms, ridge_weight, inverse_width):
    coef_whole = lax.all_gather(direction, "pts", axis=0, tiled=True).astype(jnp.bfloat16)
    local_rows = points.shape[0]
    empty = jnp.zeros((local_rows,), jnp.float32)

    def accumulate(running, shard_rows, first_row):
        coef_part = lax.dynamic_slice_in_dim(coef_whole, first_row, shard_rows.shape[0], 0)
        return running + kernel_times(points, own_norms, shard_rows, coef_part, inverse_width)

    summed = over_all(points, "pts", 0, accumulate, empty)
    return summed + ridge_weight * direction


def body(points, targets, ridge_weight):
    inverse_width = 1.0 / points.shape[1]
    widened = points.astype(jnp.float32)
    own_norms = jnp.sum(widened * widened, axis=1)
    coefficients = jnp.zeros_like(targets)
    residual = targets
    direction = targets
    norm_now = lax.psum(jnp.sum(residual * residual), "pts")
    for iteration in range(ITERS):
        applied = apply_operator(direction, points, own_norms, ridge_weight, inverse_width)
        curvature = lax.psum(jnp.sum(direction * applied), "pts")
        step_size = norm_now / curvature
        coefficients = coefficients + step_size * direction
        residual = residual - step_size * applied
        if iteration + 1 < ITERS:
            norm_next = lax.psum(jnp.sum(residual * residual), "pts")
            direction = residual + norm_next / norm_now * direction
            norm_now = norm_next
    return (coefficients, residual)


def solution(mesh):
    in_specs = (P("pts", None), P("pts"), P())
    out_specs = (P("pts"), P("pts"))
    return jax.shard_map(body, mesh=mesh, in_specs=in_specs, out_specs=out_specs, check_vma=False)
```

profile of v0, /device:TPU:1, one launch (start us, length us, event | category | flops | bytes accessed | tf_op | source)
XLA Modules:
  0.0 421.1 jit_solution(7637829127541475642)
XLA Ops:
  7.2 0.0 all-gather.4.cloned.1.call-start
  7.2 0.7 all-gather.4.cloned.1.call-update
  7.9 0.7 convert
  9.2 38.9 %all-gather = bf16[128,1,512]{2,1,0:T(2,128)(2,1)S(1)} all-gather(bf16[1,1,512]{2,1,0:T(2,128)(2,1)S(1)} %convert), channel_id=1, replica_groups=mesh['pts'=128] {'pts'}, dimensions={0}, use_global_device_ids=true | all-gather | bytes 132096 | tf_op jit(solution)/shard_map/all_gather | solution.py:24
  48.1 0.9 multiply_reduce_fusion.1
  49.0 39.0 %all-gather.4.cloned.1.call-done = bf16[65536,64]{0,1:T(8,128)(2,1)} async-done(((bf16[512,64]{0,1:T(8,128)(2,1)}), bf16[65536,64]{0,1:T(8,128)(2,1)}) %all-gather.4.cloned.1.call-update) | async-done | bytes 8388624 | tf_op jit(solution)/shard_map/all_gather | solution.py:10
  88.0 5.4 %multiply_reduce_fusion = f32[65536]{0:T(1024)S(1)} fusion(bf16[65536,64]{0,1:T(8,128)(2,1)} %all-gather.4.cloned.1.call-done), kind=kLoop, calls=%fused_computation.1 | loop fusion | flops 12517376 | bytes 8650752 | tf_op jit(solution)/shard_map/reduce_sum | solution.py:16
  93.4 36.7 %exponential_convert_fusion = bf16[512,65536]{1,0:T(8,128)(2,1)} fusion(bf16[512,64]{0,1:T(8,128)(2,1)} %param.3, bf16[65536,64]{0,1:T(8,128)(2,1)} %all-gather.4.cloned.1.call-done, f32[65536]{0:T(1024)S(1)} %multiply_reduce_fusion, f32[512]{0:T(512)S(1)} %multiply_reduce_fusion.1), kind=kOutput, calls=%fused_computation | convolution fusion | flops 4462739456 | bytes 75827200 | tf_op jit(solution)/shard_map/dot_general | solution.py:17
  130.1 0.0 copy-start
  130.1 26.6 %fusion = f32[1,512]{1,0:T(1,128)S(1)} fusion(bf16[512,65536]{1,0:T(8,128)(2,1)} %exponential_convert_fusion, bf16[65536,1]{0,1:T(2,128)(2,1)S(1)} %bitcast.12), kind=kOutput, calls=%fused_computation.13 | convolution fusion | flops 67108864 | bytes 67241984 | tf_op jit(solution)/shard_map/dot_general | solution.py:20
  156.7 0.0 copy-done
  156.7 0.6 multiply_reduce_fusion.4
  157.3 64.5 %all-reduce = (f32[]{:T(128)}, f32[]{:T(128)}) all-reduce(f32[]{:T(128)} %get-tuple-element.3, f32[]{:T(128)} %get-tuple-element.2), channel_id=1, replica_groups=mesh['pts'=128] {'pts'}, use_global_device_ids=true, to_apply=%region_1.0 | all-reduce | flops 2 | bytes 16 | tf_op jit(solution)/shard_map/psum | solution.py:43
  223.1 0.6 multiply_reduce_fusion.3
  223.7 63.8 %psum.30 = f32[]{:T(128)} all-reduce(f32[]{:T(128)} %multiply_reduce_fusion.3), channel_id=1, replica_groups=mesh['pts'=128] {'pts'}, use_global_device_ids=true, to_apply=%region_7.0 | all-reduce | flops 1 | bytes 8 | tf_op jit(solution)/shard_map/psum | solution.py:51
  288.9 34.1 %all-gather.1 = bf16[128,1,512]{2,1,0:T(2,128)(2,1)S(1)} all-gather(bf16[1,1,512]{2,1,0:T(2,128)(2,1)S(1)} %convert.1), channel_id=1, replica_groups=mesh['pts'=128] {'pts'}, dimensions={0}, use_global_device_ids=true | all-gather | bytes 132096 | tf_op jit(solution)/shard_map/all_gather | solution.py:24
  323.0 26.6 %fusion.1 = f32[1,512]{1,0:T(1,128)S(1)} fusion(bf16[512,65536]{1,0:T(8,128)(2,1)} %exponential_convert_fusion, bf16[65536,1]{0,1:T(2,128)(2,1)S(1)} %bitcast.13), kind=kOutput, calls=%fused_computation.14 | convolution fusion | flops 67108864 | bytes 67241984 | tf_op jit(solution)/shard_map/dot_general | solution.py:20
  349.6 0.6 multiply_reduce_fusion.2
  350.2 62.1 %psum.31 = f32[]{:T(128)} all-reduce(f32[]{:T(128)} %multiply_reduce_fusion.2), channel_id=1, replica_groups=mesh['pts'=128] {'pts'}, use_global_device_ids=true, to_apply=%region_9.0 | all-reduce | flops 1 | bytes 8 | tf_op jit(solution)/shard_map/psum | solution.py:46
  413.7 0.6 multiply_subtract_fusion
  (2 shorter events, 0.0 us)
Async XLA Ops:
  7.2 80.8 %all-gather.4.cloned.1.call-start = ((), (), s32[]{:S(2)}) async-start(), calls=%async_computation | async-start | bytes 8454144 | tf_op jit(solution)/shard_map/all_gather | solution.py:10
  130.1 26.6 %copy-start = (f32[512]{0:T(512)S(1)}, f32[512]{0:T(512)}, u32[]{:S(2)}) copy-start(f32[512]{0:T(512)} %param.4) | copy-start | bytes 6148
Sparse Core Ops, SparseCore 0:
  10.8 77.1 all-gather.3
where the time goes:
time: 422 us; the launch traced here: 421 us
  blocking collectives  263 us (62%)
  matrix products  89.8 us (21%)
  waiting for transfers between devices  39.7 us (9%)
  between operations  18.7 us (4%)
  other arithmetic  9.44 us (2%)
    all_gather x2, blocking collectives, apply_operator(): lax.all_gather(direction, 'pts', axis=0, tiled=True).astype(jnp.bfloat16)  73 us
    psum x1, blocking collectives, body(): norm_now = lax.psum(jnp.sum(residual * residual), 'pts')  64.5 us
    psum x1, blocking collectives, body(): norm_next = lax.psum(jnp.sum(residual * residual), 'pts')  63.8 us
    psum x1, blocking collectives, body(): curvature = lax.psum(jnp.sum(direction * applied), 'pts')  62.1 us
    dot_general x2, matrix products, kernel_times(): return jnp.dot(kernel, coef_part, preferred_element_type=jnp.float32)  53.2 us
    all_gather x1, waiting for transfers between devices, over_all(): lax.all_gather(a, axis, axis=dim, tiled=True)  39 us
    dot_general x1, matrix products, kernel_times(): jnp.dot(own_points, shard_rows.T, preferred_element_type=jnp.float32)  36.7 us
  transfers between devices with their start and end apart: 1, of which 1 were waited for; matrix products, arithmetic and copies ran while one was open for 0% of the time, Pallas kernels for 0%

commit v1 on v0

--- a/solution.py
+++ b/solution.py
@@ -21,7 +21,9 @@
 
 
 def apply_operator(direction, points, own_norms, ridge_weight, inverse_width):
-    coef_whole = lax.all_gather(direction, "pts", axis=0, tiled=True).astype(jnp.bfloat16)
+    coef_whole = jnp.concatenate(
+        lax.all_to_all(jnp.stack([direction] * lax.axis_size("pts")), "pts", 0, 0), axis=0
+    ).astype(jnp.bfloat16)
     local_rows = points.shape[0]
     empty = jnp.zeros((local_rows,), jnp.float32)
 

time: 422 us -> 405 us (0.960)
  blocking collectives: 263 us -> 206 us
  waiting for transfers between devices: 39.7 us -> 64.3 us
  starting transfers between devices: 0.04 us -> 11.5 us
    all_gather x2 -> x0, blocking collectives: 73 us -> none  [apply_operator(): lax.all_gather(direction, 'pts', axis=0, tiled=True).astype(jnp.bfloat16)]
    all_gather x1, waiting for transfers between devices: 39 us -> 55.1 us  [over_all(): lax.all_gather(a, axis, axis=dim, tiled=True)]
    all_to_all x0 -> x1, blocking collectives: none -> 14.6 us  [apply_operator(): lax.all_to_all(jnp.stack([direction] * lax.axis_size('pts')), 'pts', 0, 0)]
    all_to_all x0 -> x1, starting transfers between devices: none -> 11.5 us  [apply_operator(): lax.all_to_all(jnp.stack([direction] * lax.axis_size('pts')), 'pts', 0, 0)]
    all_to_all x0 -> x1, waiting for transfers between devices: none -> 8.49 us  [apply_operator(): lax.all_to_all(jnp.stack([direction] * lax.axis_size('pts')), 'pts', 0, 0)]
  transfers between devices with their start and end apart: 1 -> 2, of which waited for: 1 -> 2; matrix products, arithmetic and copies ran while one was open for 0% -> 1% of each run, Pallas kernels for 0% -> 0%
where the time goes in v1:
time: 405 us; the launch traced here: 404 us
  blocking collectives  206 us (51%)
  matrix products  89.8 us (22%)
  waiting for transfers between devices  64.3 us (16%)
  between operations  18.8 us (5%)
  other arithmetic  11.6 us (3%)
  starting transfers between devices  11.5 us (3%)
    psum x1, blocking collectives, body(): norm_now = lax.psum(jnp.sum(residual * residual), 'pts')  64.5 us
    psum x1, blocking collectives, body(): norm_next = lax.psum(jnp.sum(residual * residual), 'pts')  63.8 us
    psum x1, blocking collectives, body(): curvature = lax.psum(jnp.sum(direction * applied), 'pts')  62.8 us
    all_gather x1, waiting for transfers between devices, over_all(): lax.all_gather(a, axis, axis=dim, tiled=True)  55.1 us
    dot_general x2, matrix products, kernel_times(): return jnp.dot(kernel, coef_part, preferred_element_type=jnp.float32)  53.2 us
    dot_general x1, matrix products, kernel_times(): jnp.dot(own_points, shard_rows.T, preferred_element_type=jnp.float32)  36.6 us
    all_to_all x1, blocking collectives, apply_operator(): lax.all_to_all(jnp.stack([direction] * lax.axis_size('pts')), 'pts', 0, 0)  14.6 us
    all_to_all x1, starting transfers between devices, apply_operator(): lax.all_to_all(jnp.stack([direction] * lax.axis_size('pts')), 'pts', 0, 0)  11.5 us
  transfers between devices with their start and end apart: 2, of which 2 were waited for; matrix products, arithmetic and copies ran while one was open for 1% of the time, Pallas kernels for 0%

profile of v1, /device:TPU:1, one launch (start us, length us, event | category | flops | bytes accessed | tf_op | source)
XLA Modules:
  0.0 404.0 jit_solution(10644098647447051688)
XLA Ops:
  7.2 0.0 all-gather.2.cloned.1.call-start
  7.2 0.7 all-gather.2.cloned.1.call-update
  7.9 0.8 stack.4
  8.7 0.5 broadcast.20
  9.2 1.4 reduce
  10.6 0.7 reshape.32
  11.3 11.5 %all-to-all-start = ((bf16[128,2,256]{2,1,0:T(2,128)(2,1)}), bf16[128,2,256]{2,1,0:T(2,128)(2,1)S(1)}, u32[]{:S(2)}, u32[]{:S(2)}) async-start(bf16[128,2,256]{2,1,0:T(2,128)(2,1)} %reshape.32), calls=%async_computation | async-start | bytes 262144 | tf_op jit(solution)/shard_map/all_to_all | solution.py:25
  23.5 0.9 multiply_reduce_fusion.1
  24.3 8.5 %all-to-all-done = bf16[128,2,256]{2,1,0:T(2,128)(2,1)S(1)} async-done(((bf16[128,2,256]{2,1,0:T(2,128)(2,1)}), bf16[128,2,256]{2,1,0:T(2,128)(2,1)S(1)}, u32[]{:S(2)}, u32[]{:S(2)}) %all-to-all-start) | async-done | bytes 131104 | tf_op jit(solution)/shard_map/all_to_all | solution.py:25
  32.8 0.1 reshape.33
  32.9 55.1 %all-gather.2.cloned.1.call-done = bf16[65536,64]{0,1:T(8,128)(2,1)} async-done(((bf16[512,64]{0,1:T(8,128)(2,1)}), bf16[65536,64]{0,1:T(8,128)(2,1)}) %all-gather.2.cloned.1.call-update) | async-done | bytes 8388624 | tf_op jit(solution)/shard_map/all_gather | solution.py:10
  88.0 5.4 %multiply_reduce_fusion = f32[65536]{0:T(1024)S(1)} fusion(bf16[65536,64]{0,1:T(8,128)(2,1)} %all-gather.2.cloned.1.call-done), kind=kLoop, calls=%fused_computation.1 | loop fusion | flops 12517376 | bytes 8650752 | tf_op jit(solution)/shard_map/reduce_sum | solution.py:16
  93.4 36.6 %exponential_convert_fusion = bf16[512,65536]{1,0:T(8,128)(2,1)} fusion(bf16[512,64]{0,1:T(8,128)(2,1)} %param.3, bf16[65536,64]{0,1:T(8,128)(2,1)} %all-gather.2.cloned.1.call-done, f32[65536]{0:T(1024)S(1)} %multiply_reduce_fusion, f32[512]{0:T(512)S(1)} %multiply_reduce_fusion.1), kind=kOutput, calls=%fused_computation | convolution fusion | flops 4462739456 | bytes 75827200 | tf_op jit(solution)/shard_map/dot_general | solution.py:17
  130.1 0.0 copy-start
  130.1 26.6 %fusion = f32[1,512]{1,0:T(1,128)S(1)} fusion(bf16[512,65536]{1,0:T(8,128)(2,1)} %exponential_convert_fusion, bf16[65536,1]{0,1:T(2,128)(2,1)S(1)} %bitcast.10), kind=kOutput, calls=%fused_computation.13 | convolution fusion | flops 67108864 | bytes 67241984 | tf_op jit(solution)/shard_map/dot_general | solution.py:20
  156.7 0.0 copy-done
  156.7 0.6 multiply_reduce_fusion.4
  157.3 64.5 %all-reduce = (f32[]{:T(128)}, f32[]{:T(128)}) all-reduce(f32[]{:T(128)} %get-tuple-element.3, f32[]{:T(128)} %get-tuple-element.2), channel_id=1, replica_groups=mesh['pts'=128] {'pts'}, use_global_device_ids=true, to_apply=%region_1.0 | all-reduce | flops 2 | bytes 16 | tf_op jit(solution)/shard_map/psum | solution.py:45
  223.2 0.6 multiply_reduce_fusion.3
  223.8 63.8 %psum.30 = f32[]{:T(128)} all-reduce(f32[]{:T(128)} %multiply_reduce_fusion.3), channel_id=1, replica_groups=mesh['pts'=128] {'pts'}, use_global_device_ids=true, to_apply=%region_7.0 | all-reduce | flops 1 | bytes 8 | tf_op jit(solution)/shard_map/psum | solution.py:53
  289.0 0.1 stack.5
  289.1 1.4 reduce.1
  290.6 14.6 %all_to_all.12 = bf16[128,2,256]{2,1,0:T(2,128)(2,1)S(1)} all-to-all(bf16[128,2,256]{2,1,0:T(2,128)(2,1)S(1)} %reshape.34), channel_id=1, replica_groups=mesh['pts'=128] {'pts'}, dimensions={0} | all-to-all | bytes 262144 | tf_op jit(solution)/shard_map/all_to_all | solution.py:25
  305.2 0.1 reshape.35
  305.3 26.6 %fusion.1 = f32[1,512]{1,0:T(1,128)S(1)} fusion(bf16[512,65536]{1,0:T(8,128)(2,1)} %exponential_convert_fusion, bf16[65536,1]{0,1:T(2,128)(2,1)S(1)} %bitcast.11), kind=kOutput, calls=%fused_computation.14 | convolution fusion | flops 67108864 | bytes 67241984 | tf_op jit(solution)/shard_map/dot_general | solution.py:20
  331.9 0.6 multiply_reduce_fusion.2
  332.5 62.8 %psum.31 = f32[]{:T(128)} all-reduce(f32[]{:T(128)} %multiply_reduce_fusion.2), channel_id=1, replica_groups=mesh['pts'=128] {'pts'}, use_global_device_ids=true, to_apply=%region_9.0 | all-reduce | flops 1 | bytes 8 | tf_op jit(solution)/shard_map/psum | solution.py:48
  396.6 0.6 multiply_subtract_fusion
  (2 shorter events, 0.0 us)
Async XLA Ops:
  7.2 80.8 %all-gather.2.cloned.1.call-start = ((), (), s32[]{:S(2)}) async-start(), calls=%async_computation.2 | async-start | bytes 8454144 | tf_op jit(solution)/shard_map/all_gather | solution.py:10
  11.3 21.5 %all-to-all-start = ((bf16[128,2,256]{2,1,0:T(2,128)(2,1)}), bf16[128,2,256]{2,1,0:T(2,128)(2,1)S(1)}, u32[]{:S(2)}, u32[]{:S(2)}) async-start(bf16[128,2,256]{2,1,0:T(2,128)(2,1)} %reshape.32), calls=%async_computation | async-start | bytes 262144 | tf_op jit(solution)/shard_map/all_to_all | solution.py:25
  130.1 26.6 %copy-start = (f32[512]{0:T(512)S(1)}, f32[512]{0:T(512)}, u32[]{:S(2)}) copy-start(f32[512]{0:T(512)} %param.4) | copy-start | bytes 6148
Sparse Core Ops, SparseCore 0:
  10.8 77.1 all-gather.1
